TPU v7x, 32 devices: a whole 2x2x4 slice. The times are simulated.
32 devices in a mesh: blk: 8 (over y, x, core), uly: 4 (over z).
Axes of the slice: x: 2, y: 2, z: 4, core: 2. Of those that a mesh axis runs over, the one named last changes fastest.
Arguments:
- queries: bfloat16 [4096, 4096], P(('blk', 'uly')), may hold values from -100 to 100
- keys: bfloat16 [4096, 512], P(('blk', 'uly')), may hold values from -6 to 6
- values: bfloat16 [4096, 512], P(('blk', 'uly')), may hold values from -6 to 6
- segments: int32 [4096], P(('blk', 'uly')), may hold values from 0 to 7, never falling along the last dimension, each value on 1 to 2048 neighbouring positions
Outputs:
- attended: bfloat16 [4096, 4096], P(('blk', 'uly'))
Inputs may be any that keep to these rules, and one draw needn't show every extreme that they name: `segments`: document numbers never fall along the sequence; each document holds 1 to 2048 positions.
All inputs are finite; a program needn't handle non-finite values.
Results may differ from a plain program's by a relative error of at most 0.0039.
Values may be sent and summed in bfloat16 or wider, within the bound.
No kernel may reach another device: no remote copies, remote signals or barrier semaphores. Data moves between devices by JAX's collectives and lax.ppermute only.
A program may use at most 64 MiB of HBM per device.

v0:
```python
import functools

import jax
import jax.numpy as jnp
from jax import lax
from jax.experimental import pallas as pl
from jax.experimental.pallas import tpu as pltpu
from jax.sharding import Mesh
from jax.sharding import PartitionSpec as P


HEAD_SIZE = 128
DOCUMENTS = 8
LOG2E = 1.4426950408889634
LOW = -1e30
AXES = ("outer", "group", "core", "uly")
VMEM = pl.BlockSpec(memory_space=pltpu.VMEM)
HBM = pl.BlockSpec(memory_space=pltpu.HBM)


def pack(k_ref, v_ref, seg_ref, *rest, groups):
    out, (k_buf, v_buf, seg_buf, sems) = rest[:groups], rest[groups:]
    rows = k_buf.shape[0]
    mine = lax.axis_index("group")
    pairs = ((seg_ref, seg_buf), (k_ref, k_buf), (v_ref, v_buf))
    copies = [pltpu.make_async_copy(x, y, sems.at[i]) for i, (x, y) in enumerate(pairs)]
    for copy in copies:
        copy.start()
    copies[0].wait()
    number = lax.broadcasted_iota(jnp.int32, (DOCUMENTS, rows), 0)
    below = jnp.where(seg_buf[...] < number, 1.0, 0.0)
    counts = jnp.broadcast_to(jnp.sum(below, axis=1, keepdims=True), (DOCUMENTS, HEAD_SIZE)).astype(jnp.bfloat16)
    copies[1].wait()
    copies[2].wait()
    for i in range(groups):
        cut = pl.ds(pl.multiple_of((mine ^ i) * HEAD_SIZE, HEAD_SIZE), HEAD_SIZE)
        out[i][:rows, :] = k_buf[:, cut]
        out[i][rows : 2 * rows, :] = v_buf[:, cut]
        out[i][2 * rows :, :] = counts


def pack_queries(q_ref, *rest, groups):
    out, sems = rest[:groups], rest[groups]
    width = out[0].shape[1]
    mine = lax.axis_index("group")
    copies = []
    for i in range(groups):
        start = pl.multiple_of((mine ^ i) * width, width)
        copies.append(pltpu.make_async_copy(q_ref.at[:, pl.ds(start, width)], out[i], sems.at[i]))
        copies[-1].start()
    for copy in copies:
        copy.wait()


def merge(*refs, groups):
    pieces, out_ref = refs[:groups], refs[groups]
    mine = lax.axis_index("group")
    for i in range(groups):
        out_ref[mine ^ i] = pieces[i][...]


def attend(*refs, index, turns, rows, groups, layers, split, sides, resume, final):
    count = len(turns)
    q_ref, home_ref = refs[:2]
    refs = refs[2:]
    tiles = []
    for side in sides:
        tiles.append(refs[:count] if side else ())
        refs = refs[len(tiles[-1]) :]
    own, mate = tiles
    state, refs = (refs[:3], refs[3:]) if resume else (None, refs)
    out_ref, held = (refs[0], refs[1:]) if final else (None, refs)
    m_ref, l_ref, acc_ref, s_ref = held
    per = q_ref.shape[1] // HEAD_SIZE
    chips = home_ref.shape[0]
    scale = HEAD_SIZE ** -0.5 * LOG2E
    core, layer = lax.axis_index("core"), lax.axis_index("uly")
    home = lax.axis_index("outer") * groups + (lax.axis_index("group") ^ index)
    shape = (rows, HEAD_SIZE)
    lane = lax.broadcasted_iota(jnp.int32, (DOCUMENTS, HEAD_SIZE), 1).astype(jnp.float32)
    number = lax.broadcasted_iota(jnp.int32, (DOCUMENTS, HEAD_SIZE), 0).astype(jnp.float32)

    def counts(ref, chip):
        return ref[chip, 2 * rows :, :].astype(jnp.float32)

    mine = counts(home_ref, home)
    local_row = lax.broadcasted_iota(jnp.int32, shape, 0).astype(jnp.float32)
    row_doc = jnp.zeros(shape, jnp.float32)
    for d in range(DOCUMENTS):
        row_doc = row_doc + jnp.where(jnp.broadcast_to(mine[d : d + 1], shape) <= local_row, 1.0, 0.0)
    place = ((home * 2 + core) * layers + layer) * rows + lax.broadcasted_iota(jnp.int32, shape, 0)
    earliest = row_doc[:1] - 1.0

    def skipped(tiles):
        gone = jnp.zeros((1, HEAD_SIZE), jnp.float32)
        for chip in range(chips):
            least = None
            for ref in tiles:
                held_below = jnp.sum(jnp.where(number == earliest, counts(ref, chip), 0.0), axis=0, keepdims=True)
                least = held_below if least is None else jnp.minimum(least, held_below)
            gone = gone + jnp.where(least >= rows, 1.0, 0.0)
        return jnp.max(gone).astype(jnp.int32)

    m_ref[...] = jnp.full(m_ref.shape, LOW, jnp.float32)
    part = per // split
    heads = list(range(per))
    last_own, last_mate = home + 1, home + core
    first_own = skipped(own) if own else last_own
    first_mate = skipped(mate) if mate else last_mate
    second = last_own - first_own

    def strip(h):
        return pl.ds(h * rows, rows)

    def score(tiles, chip, parity, slot):
        k = jnp.concatenate([ref[chip, :rows, :] for ref in tiles], axis=0)
        bias = []
        for turn, ref in zip(turns, tiles):
            base = ((chip * 2 + parity) * layers + (layer ^ turn)) * rows
            key_doc = jnp.sum(jnp.where(counts(ref, chip) <= lane, 1.0, 0.0), axis=0, keepdims=True)
            key = base + lax.broadcasted_iota(jnp.int32, shape, 1)
            bias.append(jnp.where((key <= place) & (row_doc == key_doc), 0.0, LOW))
        for h0 in range(0, per, part):
            q = jnp.concatenate([q_ref[:, h * HEAD_SIZE : (h + 1) * HEAD_SIZE] for h in heads[h0 : h0 + part]], axis=0)
            s = lax.dot_general(q, k, (((1,), (1,)), ((), ())), preferred_element_type=jnp.float32)
            for i in range(part):
                xs = [s[i * rows : (i + 1) * rows, c * rows : (c + 1) * rows] + bias[c] for c in range(count)]
                for c in range(count):
                    s_ref[slot, strip(h0 + i), c * rows : (c + 1) * rows] = xs[c]
                m_ref[strip(h0 + i), :] = functools.reduce(jnp.maximum, xs, m_ref[strip(h0 + i), :])

    def weigh(tiles, chip, slot):
        v = jnp.concatenate([ref[chip, rows : 2 * rows, :] for ref in tiles], axis=0)
        for h0 in range(0, per, part):
            ps = []
            for h in heads[h0 : h0 + part]:
                shift = m_ref[strip(h), :]
                p = [
                    jnp.exp2(s_ref[slot, strip(h), c * rows : (c + 1) * rows] * scale - shift) for c in range(count)
                ]
                l_ref[strip(h), :] = functools.reduce(jnp.add, p, l_ref[strip(h), :])
                ps.append(jnp.concatenate([y.astype(jnp.bfloat16) for y in p], axis=1))
            pv = lax.dot_general(
                jnp.concatenate(ps, axis=0), v, (((1,), (0,)), ((), ())), preferred_element_type=jnp.float32
            )
            r = pl.ds(h0 * rows, part * rows)
            acc_ref[r, :] = acc_ref[r, :] + pv

    if own:

        @pl.loop(first_own, last_own)
        def _(chip):
            score(own, chip, core, chip - first_own)

    if mate:

        @pl.loop(first_mate, last_mate)
        def _(chip):
            score(mate, chip, 1 - core, second + chip - first_mate)

    for h in heads:
        r = strip(h)
        top = jnp.broadcast_to(jnp.max(m_ref[r, :], axis=1, keepdims=True) * scale, shape)
        if resume:
            old = state[0][r, :]
            top = jnp.maximum(top, old)
            factor = jnp.exp2(old - top)
            l_ref[r, :] = state[1][r, :] * factor
            acc_ref[r, :] = state[2][r, :] * factor
        else:
            l_ref[r, :] = jnp.zeros(shape, jnp.float32)
            acc_ref[r, :] = jnp.zeros(shape, jnp.float32)
        m_ref[r, :] = top

    if own:

        @pl.loop(first_own, last_own)
        def _(chip):
            weigh(own, chip, chip - first_own)

    if mate:

        @pl.loop(first_mate, last_mate)
        def _(chip):
            weigh(mate, chip, second + chip - first_mate)

    if final:
        for h in heads:
            r = strip(h)
            total = jnp.sum(l_ref[r, :], axis=1, keepdims=True)
            out_ref[:, h * HEAD_SIZE : (h + 1) * HEAD_SIZE] = (acc_ref[r, :] / total).astype(out_ref.dtype)


def place(*refs, turns):
    pieces, out_ref, sems = refs[: len(turns)], refs[-2], refs[-1]
    width = pieces[0].shape[1]
    mine = lax.axis_index("group")
    copies = []
    for i, piece in zip(turns, pieces):
        start = pl.multiple_of((mine ^ i) * width, width)
        copies.append(pltpu.make_async_copy(piece, out_ref.at[:, pl.ds(start, width)], sems.at[i]))
        copies[-1].start()
    for copy in copies:
        copy.wait()


def limit(mib):
    return pltpu.CompilerParams(vmem_limit_bytes=mib << 20)


def local(queries, keys, values, segments, *, outer, groups, layers):
    rows = queries.shape[0]
    width = queries.shape[1] // groups
    per = width // HEAD_SIZE
    piece = jax.ShapeDtypeStruct((rows, width), jnp.bfloat16)
    one = jax.ShapeDtypeStruct((2 * rows + DOCUMENTS, HEAD_SIZE), jnp.bfloat16)
    raw = [pltpu.with_memory_space_constraint(x, pltpu.HBM) for x in (keys, values, segments.reshape(1, rows), queries)]
    kv = list(
        pl.pallas_call(
            functools.partial(pack, groups=groups),
            out_shape=[one] * groups,
            in_specs=[HBM] * 3,
            out_specs=[VMEM] * groups,
            scratch_shapes=[
                pltpu.VMEM(keys.shape, jnp.bfloat16),
                pltpu.VMEM(values.shape, jnp.bfloat16),
                pltpu.VMEM((1, rows), jnp.int32),
                pltpu.SemaphoreType.DMA((3,)),
            ],
            compiler_params=limit(4),
            name="pack",
        )(*raw[:3])
    )
    q = list(
        pl.pallas_call(
            functools.partial(pack_queries, groups=groups),
            out_shape=[piece] * groups,
            in_specs=[HBM],
            out_specs=[VMEM] * groups,
            scratch_shapes=[pltpu.SemaphoreType.DMA((groups,))],
            compiler_params=limit(4),
            name="pack_queries",
        )(raw[3])
    )

    def swap(x, axis, size, i):
        return lax.ppermute(x, axis, [(g, g ^ i) for g in range(size)])

    order = list(range(groups - 1, 0, -1))
    for i in order:
        kv[i] = swap(kv[i], "group", groups, i)
    for i in order:
        q[i] = swap(q[i], "group", groups, i)
    mine = pl.pallas_call(
        functools.partial(merge, groups=groups),
        out_shape=jax.ShapeDtypeStruct((groups, *one.shape), jnp.bfloat16),
        in_specs=[VMEM] * groups,
        out_specs=VMEM,
        compiler_params=limit(4),
        name="merge",
    )(*kv)
    if outer > 1:
        mine = lax.all_gather(mine, "outer", axis=0, tiled=True)
    own = [mine] + [swap(mine, "uly", layers, j) for j in range(1, layers)]
    mate = []
    for j in range(layers):
        mate.append(lax.ppermute(own[j], "core", [(0, 1), (1, 0)]))

    held = [jax.ShapeDtypeStruct((per * rows, HEAD_SIZE), jnp.float32)] * 3
    common = dict(rows=rows, groups=groups, layers=layers, split=2)
    units = 2 * (outer * groups // 2 + 1)
    near, far = list(range(layers // 2)), list(range(layers // 2, layers))

    def call(i, turns, sides, state, final):
        args = [q[i], own[0]]
        for side, held_by in zip(sides, (own, mate)):
            args += [held_by[j] for j in turns] if side else []
        args += state or []
        keep = dict(sides=sides, resume=state is not None, final=final)
        return pl.pallas_call(
            functools.partial(attend, index=i, turns=turns, **keep, **common),
            out_shape=piece if final else held,
            in_specs=[VMEM] * len(args),
            out_specs=VMEM if final else [VMEM] * 3,
            scratch_shapes=([pltpu.VMEM(x.shape, x.dtype) for x in held] if final else [])
            + [pltpu.VMEM((units, per * rows, len(turns) * rows), jnp.float32)],
            compiler_params=limit(8 + units),
            name="attend",
        )(*args)

    both, states, out, last = (True, True), [None] * groups, [None] * groups, None

    def follow(i):
        nonlocal last
        if last is not None:
            q[i], last = lax.optimization_barrier((q[i], last))

    for i in [0] + order:
        follow(i)
        states[i] = call(i, near, both, None, False)
        last = states[i][0]
    i = order[0]
    follow(i)
    states[i] = call(i, far, (True, False), states[i], False)
    last = states[i][0]
    for i in order + [0]:
        follow(i)
        last = call(i, far, (False, True) if i == order[0] else both, states[i], True)
        out[i] = swap(last, "group", groups, i) if i else last

    def put(turns, *rest):
        return pl.pallas_call(
            functools.partial(place, turns=turns),
            out_shape=jax.ShapeDtypeStruct(queries.shape, jnp.bfloat16),
            in_specs=[VMEM] * len(turns) + [HBM] * len(rest),
            out_specs=HBM,
            scratch_shapes=[pltpu.SemaphoreType.DMA((groups,))],
            input_output_aliases={len(turns): 0} if rest else {},
            compiler_params=limit(4),
            name="place",
        )(*(out[i] for i in turns), *rest)

    return put(order[-1:], put([0] + order[:-1]))


def solution(mesh):
    blocks, layers = mesh.shape["blk"], mesh.shape["uly"]

    def run(queries, keys, values, segments):
        groups = keys.shape[1] // HEAD_SIZE
        outer = blocks // 2 // groups
        fine = Mesh(mesh.devices.reshape(outer, groups, 2, layers), AXES)

        def body(*args):
            return local(*args, outer=outer, groups=groups, layers=layers)

        spec = P(AXES)
        step = jax.shard_map(body, mesh=fine, in_specs=(spec,) * 4, out_specs=spec, check_vma=False)
        return step(queries, keys, values, segments)

    return run
```

profile of v0, /device:TPU:17, one launch (start us, length us, event | category | flops | bytes accessed | tf_op | source)
XLA Modules:
  0.0 75.6 jit_solution(7032011560040062215)
XLA Ops:
  1.1 1.3 %collective-permute-start.3 = (bf16[264,128]{1,0:T(8,128)(2,1)S(1)}, bf16[264,128]{1,0:T(8,128)(2,1)S(1)}, u32[]{:S(2)}, u32[]{:S(2)}) collective-permute-start(bf16[264,128]{1,0:T(8,128)(2,1)S(1)} %get-tuple-element.41), channel_id=1, source_target_pairs={{0,8},{8,0},{16,24},{24,16},{1,9},{9,1},{17,25},{25,17},{2,10},{10... | collective-permute-start | bytes 202760 | tf_op jit(solution)/shard_map/ppermute | solution.py:247
  2.3 1.2 %collective-permute-start.4 = (bf16[264,128]{1,0:T(8,128)(2,1)S(1)}, bf16[264,128]{1,0:T(8,128)(2,1)S(1)}, u32[]{:S(2)}, u32[]{:S(2)}) collective-permute-start(bf16[264,128]{1,0:T(8,128)(2,1)S(1)} %get-tuple-element.42), channel_id=1, source_target_pairs={{0,16},{8,24},{16,0},{24,8},{1,17},{9,25},{17,1},{25,9},{2,18},{10... | collective-permute-start | bytes 202760 | tf_op jit(solution)/shard_map/ppermute | solution.py:247
  4.3 1.4 %collective-permute-done.4.refs_2_ = bf16[264,128]{1,0:T(8,128)(2,1)S(1)} collective-permute-done((bf16[264,128]{1,0:T(8,128)(2,1)S(1)}, bf16[264,128]{1,0:T(8,128)(2,1)S(1)}, u32[]{:S(2)}, u32[]{:S(2)}) %collective-permute-start.4) | collective-permute-done | bytes 67616 | tf_op jit(solution)/shard_map/ppermute | solution.py:247
  5.7 1.9 %collective-permute-done.5.refs_3_ = bf16[264,128]{1,0:T(8,128)(2,1)S(1)} collective-permute-done((bf16[264,128]{1,0:T(8,128)(2,1)S(1)}, bf16[264,128]{1,0:T(8,128)(2,1)S(1)}, u32[]{:S(2)}, u32[]{:S(2)}) %collective-permute-start.5) | collective-permute-done | bytes 67616 | tf_op jit(solution)/shard_map/ppermute | solution.py:247
  7.7 1.4 %collective-permute-start.6 = (bf16[4,264,128]{2,1,0:T(8,128)(2,1)S(1)}, bf16[4,264,128]{2,1,0:T(8,128)(2,1)S(1)}, u32[]{:S(2)}, u32[]{:S(2)}) collective-permute-start(bf16[4,264,128]{2,1,0:T(8,128)(2,1)S(1)} %merge.1.refs_1_.refs_2_), channel_id=1, source_target_pairs={{0,1},{1,0},{2,3},{3,2},{4,5},{5,4},{6,7},{7,6},{8,9},{9,8},{10,11... | collective-permute-start | bytes 811016 | tf_op jit(solution)/shard_map/ppermute | solution.py:247
  9.1 1.3 %collective-permute-start.10 = (bf16[4,264,128]{2,1,0:T(8,128)(2,1)S(1)}, bf16[4,264,128]{2,1,0:T(8,128)(2,1)S(1)}, u32[]{:S(2)}, u32[]{:S(2)}) collective-permute-start(bf16[4,264,128]{2,1,0:T(8,128)(2,1)S(1)} %merge.1.refs_1_.refs_2_), channel_id=1, source_target_pairs={{0,3},{1,2},{2,1},{3,0},{4,7},{5,6},{6,5},{7,4},{8,11},{9,10},{10,... | collective-permute-start | bytes 811016 | tf_op jit(solution)/shard_map/ppermute | solution.py:247
  10.4 3.2 %collective-permute-start.7 = (bf16[4,264,128]{2,1,0:T(8,128)(2,1)S(1)}, bf16[4,264,128]{2,1,0:T(8,128)(2,1)S(1)}, u32[]{:S(2)}, u32[]{:S(2)}) collective-permute-start(bf16[4,264,128]{2,1,0:T(8,128)(2,1)S(1)} %merge.1.refs_1_.refs_2_), channel_id=1, source_target_pairs={{0,4},{4,0},{1,5},{5,1},{2,6},{6,2},{3,7},{7,3},{8,12},{12,8},{9,1... | collective-permute-start | bytes 811016 | tf_op jit(solution)/shard_map/ppermute | solution.py:267
  13.6 4.3 %collective-permute-done.6.refs_3_ = bf16[4,264,128]{2,1,0:T(8,128)(2,1)S(1)} collective-permute-done((bf16[4,264,128]{2,1,0:T(8,128)(2,1)S(1)}, bf16[4,264,128]{2,1,0:T(8,128)(2,1)S(1)}, u32[]{:S(2)}, u32[]{:S(2)}) %collective-permute-start.6) | collective-permute-done | bytes 270368 | tf_op jit(solution)/shard_map/ppermute | solution.py:247
  17.9 2.9 %collective-permute-start.8 = (bf16[4,264,128]{2,1,0:T(8,128)(2,1)S(1)}, bf16[4,264,128]{2,1,0:T(8,128)(2,1)S(1)}, u32[]{:S(2)}, u32[]{:S(2)}) collective-permute-start(bf16[4,264,128]{2,1,0:T(8,128)(2,1)S(1)} %collective-permute-done.6.refs_3_), channel_id=1, source_target_pairs={{0,4},{4,0},{1,5},{5,1},{2,6},{6,2},{3,7},{7,3},{8,12},{12,8},{9,1... | collective-permute-start | bytes 811016 | tf_op jit(solution)/shard_map/ppermute | solution.py:267
  20.7 9.6 %collective-permute-start.11 = (bf16[4,264,128]{2,1,0:T(8,128)(2,1)S(1)}, bf16[4,264,128]{2,1,0:T(8,128)(2,1)S(1)}, u32[]{:S(2)}, u32[]{:S(2)}) collective-permute-start(bf16[4,264,128]{2,1,0:T(8,128)(2,1)S(1)} %collective-permute-done.9.refs_2_), channel_id=1, source_target_pairs={{0,4},{4,0},{1,5},{5,1},{2,6},{6,2},{3,7},{7,3},{8,12},{12,8},{9,1... | collective-permute-start | bytes 811016 | tf_op jit(solution)/shard_map/ppermute | solution.py:267
  30.3 2.2 %collective-permute-done.10.refs_3_ = bf16[4,264,128]{2,1,0:T(8,128)(2,1)S(1)} collective-permute-done((bf16[4,264,128]{2,1,0:T(8,128)(2,1)S(1)}, bf16[4,264,128]{2,1,0:T(8,128)(2,1)S(1)}, u32[]{:S(2)}, u32[]{:S(2)}) %collective-permute-start.10) | collective-permute-done | bytes 270368 | tf_op jit(solution)/shard_map/ppermute | solution.py:247
  32.5 2.7 %collective-permute-start.12 = (bf16[4,264,128]{2,1,0:T(8,128)(2,1)S(1)}, bf16[4,264,128]{2,1,0:T(8,128)(2,1)S(1)}, u32[]{:S(2)}, u32[]{:S(2)}) collective-permute-start(bf16[4,264,128]{2,1,0:T(8,128)(2,1)S(1)} %collective-permute-done.10.refs_3_), channel_id=1, source_target_pairs={{0,4},{4,0},{1,5},{5,1},{2,6},{6,2},{3,7},{7,3},{8,12},{12,8},{9,1... | collective-permute-start | bytes 811016 | tf_op jit(solution)/shard_map/ppermute | solution.py:267
  35.2 1.2 %pack_queries.1 = (bf16[128,1024]{1,0:T(8,128)(2,1)S(1)}, bf16[128,1024]{1,0:T(8,128)(2,1)S(1)}, bf16[128,1024]{1,0:T(8,128)(2,1)S(1)}, bf16[128,1024]{1,0:T(8,128)(2,1)S(1)}) custom-call(bf16[128,4096]{1,0:T(8,128)(2,1)} %q_ref.1), custom_call_target="tpu_custom_call" | custom-call | tf_op jit(solution)/shard_map/pack_queries/pallas_call | solution.py:235
  37.2 1.1 %collective-permute-start.1 = (bf16[128,1024]{1,0:T(8,128)(2,1)S(1)}, bf16[128,1024]{1,0:T(8,128)(2,1)S(1)}, u32[]{:S(2)}, u32[]{:S(2)}) collective-permute-start(bf16[128,1024]{1,0:T(8,128)(2,1)S(1)} %get-tuple-element.37), channel_id=1, source_target_pairs={{0,16},{8,24},{16,0},{24,8},{1,17},{9,25},{17,1},{25,9},{2,18},{10... | collective-permute-start | bytes 786440 | tf_op jit(solution)/shard_map/ppermute | solution.py:247
  39.2 1.6 %attend.9 = (f32[1024,128]{1,0:T(8,128)S(1)}, f32[1024,128]{1,0:T(8,128)S(1)}, f32[1024,128]{1,0:T(8,128)S(1)}) custom-call(bf16[128,1024]{1,0:T(8,128)(2,1)S(1)} %get-tuple-element.64.refs_0_, bf16[4,264,128]{2,1,0:T(8,128)(2,1)S(1)} %merge.1.refs_1_.refs_2_, bf16[4,264,128]{2,1,0:T(8,128)(2,1)S(1)} %merge.1.refs_1_.refs_2_, ...), custom_call_target="tpu_custom_call" | custom-call | tf_op jit(solution)/shard_map/attend/pallas_call | solution.py:280
  40.8 4.5 %collective-permute-done.2.refs_0_ = bf16[128,1024]{1,0:T(8,128)(2,1)S(1)} collective-permute-done((bf16[128,1024]{1,0:T(8,128)(2,1)S(1)}, bf16[128,1024]{1,0:T(8,128)(2,1)S(1)}, u32[]{:S(2)}, u32[]{:S(2)}) %collective-permute-start.2) | collective-permute-done | bytes 262176 | tf_op jit(solution)/shard_map/ppermute | solution.py:247
  46.3 4.6 %collective-permute-done.1.refs_0_ = bf16[128,1024]{1,0:T(8,128)(2,1)S(1)} collective-permute-done((bf16[128,1024]{1,0:T(8,128)(2,1)S(1)}, bf16[128,1024]{1,0:T(8,128)(2,1)S(1)}, u32[]{:S(2)}, u32[]{:S(2)}) %collective-permute-start.1) | collective-permute-done | bytes 262176 | tf_op jit(solution)/shard_map/ppermute | solution.py:247
  50.9 2.9 %attend.11 = (f32[1024,128]{1,0:T(8,128)S(1)}, f32[1024,128]{1,0:T(8,128)S(1)}, f32[1024,128]{1,0:T(8,128)S(1)}) custom-call(bf16[128,1024]{1,0:T(8,128)(2,1)S(1)} %collective-permute-done.1.refs_0_, bf16[4,264,128]{2,1,0:T(8,128)(2,1)S(1)} %merge.1.refs_1_.refs_2_, bf16[4,264,128]{2,1,0:T(8,128)(2,1)S(1)} %merge.1.refs_1_.refs_2_, ...), custom_call_target="tpu_custom_call" | custom-call | tf_op jit(solution)/shard_map/attend/pallas_call | solution.py:280
  53.8 1.6 %attend.12 = (f32[1024,128]{1,0:T(8,128)S(1)}, f32[1024,128]{1,0:T(8,128)S(1)}, f32[1024,128]{1,0:T(8,128)S(1)}) custom-call(bf16[128,1024]{1,0:T(8,128)(2,1)S(1)} %collective-permute-done.refs_0_, bf16[4,264,128]{2,1,0:T(8,128)(2,1)S(1)} %merge.1.refs_1_.refs_2_, bf16[4,264,128]{2,1,0:T(8,128)(2,1)S(1)} %merge.1.refs_1_.refs_2_, ...), custom_call_target="tpu_custom_call" | custom-call | tf_op jit(solution)/shard_map/attend/pallas_call | solution.py:280
  57.2 3.1 %attend.15 = bf16[128,1024]{1,0:T(8,128)(2,1)S(1)} custom-call(bf16[128,1024]{1,0:T(8,128)(2,1)S(1)} %collective-permute-done.1.refs_0_, bf16[4,264,128]{2,1,0:T(8,128)(2,1)S(1)} %merge.1.refs_1_.refs_2_, bf16[4,264,128]{2,1,0:T(8,128)(2,1)S(1)} %collective-permute-done.9.refs_2_, bf16[4,264,128]{2,1,0:T(8,128)(2,1)S(1)} %collective-permute-done.10.refs_3_, ...), custom_call_target="tpu_custom_call" | custom-call | tf_op jit(solution)/shard_map/attend/pallas_call | solution.py:280
  61.0 1.9 %attend.16 = bf16[128,1024]{1,0:T(8,128)(2,1)S(1)} custom-call(bf16[128,1024]{1,0:T(8,128)(2,1)S(1)} %collective-permute-done.refs_0_, bf16[4,264,128]{2,1,0:T(8,128)(2,1)S(1)} %merge.1.refs_1_.refs_2_, bf16[4,264,128]{2,1,0:T(8,128)(2,1)S(1)} %collective-permute-done.9.refs_2_, bf16[4,264,128]{2,1,0:T(8,128)(2,1)S(1)} %collective-permute-done.10.refs_3_, ...), custom_call_target="tpu_custom_call" | custom-call | tf_op jit(solution)/shard_map/attend/pallas_call | solution.py:280
  62.8 2.1 %collective-permute-start.13 = (bf16[128,1024]{1,0:T(8,128)(2,1)S(1)}, bf16[128,1024]{1,0:T(8,128)(2,1)S(1)}, u32[]{:S(2)}, u32[]{:S(2)}) collective-permute-start(bf16[128,1024]{1,0:T(8,128)(2,1)S(1)} %attend.16), channel_id=1, source_target_pairs={{0,8},{8,0},{16,24},{24,16},{1,9},{9,1},{17,25},{25,17},{2,10},{10... | collective-permute-start | bytes 786440 | tf_op jit(solution)/shard_map/ppermute | solution.py:247
  65.0 1.8 %attend.17.refs_0_ = bf16[128,1024]{1,0:T(8,128)(2,1)S(1)} custom-call(bf16[128,1024]{1,0:T(8,128)(2,1)S(1)} %get-tuple-element.64.refs_0_, bf16[4,264,128]{2,1,0:T(8,128)(2,1)S(1)} %merge.1.refs_1_.refs_2_, bf16[4,264,128]{2,1,0:T(8,128)(2,1)S(1)} %collective-permute-done.9.refs_2_, bf16[4,264,128]{2,1,0:T(8,128)(2,1)S(1)} %collective-permute-done.10.refs_3_, ...), custom_call_target="tpu_custom_call" | custom-call | tf_op jit(solution)/shard_map/attend/pallas_call | solution.py:280
  66.8 6.8 %collective-permute-done.15.refs_2_ = bf16[128,1024]{1,0:T(8,128)(2,1)S(1)} collective-permute-done((bf16[128,1024]{1,0:T(8,128)(2,1)S(1)}, bf16[128,1024]{1,0:T(8,128)(2,1)S(1)}, u32[]{:S(2)}, u32[]{:S(2)}) %collective-permute-start.15) | collective-permute-done | bytes 262176 | tf_op jit(solution)/shard_map/ppermute | solution.py:247
  (22 shorter events, 8.7 us)
Async XLA Ops:
  1.1 3.2 %collective-permute-start.3 = (bf16[264,128]{1,0:T(8,128)(2,1)S(1)}, bf16[264,128]{1,0:T(8,128)(2,1)S(1)}, u32[]{:S(2)}, u32[]{:S(2)}) collective-permute-start(bf16[264,128]{1,0:T(8,128)(2,1)S(1)} %get-tuple-element.41), channel_id=1, source_target_pairs={{0,8},{8,0},{16,24},{24,16},{1,9},{9,1},{17,25},{25,17},{2,10},{10... | collective-permute-start | bytes 202760 | tf_op jit(solution)/shard_map/ppermute | solution.py:247
  2.3 3.4 %collective-permute-start.4 = (bf16[264,128]{1,0:T(8,128)(2,1)S(1)}, bf16[264,128]{1,0:T(8,128)(2,1)S(1)}, u32[]{:S(2)}, u32[]{:S(2)}) collective-permute-start(bf16[264,128]{1,0:T(8,128)(2,1)S(1)} %get-tuple-element.42), channel_id=1, source_target_pairs={{0,16},{8,24},{16,0},{24,8},{1,17},{9,25},{17,1},{25,9},{2,18},{10... | collective-permute-start | bytes 202760 | tf_op jit(solution)/shard_map/ppermute | solution.py:247
  3.6 4.0 %collective-permute-start.5 = (bf16[264,128]{1,0:T(8,128)(2,1)S(1)}, bf16[264,128]{1,0:T(8,128)(2,1)S(1)}, u32[]{:S(2)}, u32[]{:S(2)}) collective-permute-start(bf16[264,128]{1,0:T(8,128)(2,1)S(1)} %get-tuple-element.43), channel_id=1, source_target_pairs={{0,24},{8,16},{16,8},{24,0},{1,25},{9,17},{17,9},{25,1},{2,26},{10... | collective-permute-start | bytes 202760 | tf_op jit(solution)/shard_map/ppermute | solution.py:247
  7.7 10.2 %collective-permute-start.6 = (bf16[4,264,128]{2,1,0:T(8,128)(2,1)S(1)}, bf16[4,264,128]{2,1,0:T(8,128)(2,1)S(1)}, u32[]{:S(2)}, u32[]{:S(2)}) collective-permute-start(bf16[4,264,128]{2,1,0:T(8,128)(2,1)S(1)} %merge.1.refs_1_.refs_2_), channel_id=1, source_target_pairs={{0,1},{1,0},{2,3},{3,2},{4,5},{5,4},{6,7},{7,6},{8,9},{9,8},{10,11... | collective-permute-start | bytes 811016 | tf_op jit(solution)/shard_map/ppermute | solution.py:247
  9.0 11.7 %collective-permute-start.9 = (bf16[4,264,128]{2,1,0:T(8,128)(2,1)S(1)}, bf16[4,264,128]{2,1,0:T(8,128)(2,1)S(1)}, u32[]{:S(2)}, u32[]{:S(2)}) collective-permute-start(bf16[4,264,128]{2,1,0:T(8,128)(2,1)S(1)} %merge.1.refs_1_.refs_2_), channel_id=1, source_target_pairs={{0,2},{1,3},{2,0},{3,1},{4,6},{5,7},{6,4},{7,5},{8,10},{9,11},{10,... | collective-permute-start | bytes 811016 | tf_op jit(solution)/shard_map/ppermute | solution.py:247
  9.1 23.4 %collective-permute-start.10 = (bf16[4,264,128]{2,1,0:T(8,128)(2,1)S(1)}, bf16[4,264,128]{2,1,0:T(8,128)(2,1)S(1)}, u32[]{:S(2)}, u32[]{:S(2)}) collective-permute-start(bf16[4,264,128]{2,1,0:T(8,128)(2,1)S(1)} %merge.1.refs_1_.refs_2_), channel_id=1, source_target_pairs={{0,3},{1,2},{2,1},{3,0},{4,7},{5,6},{6,5},{7,4},{8,11},{9,10},{10,... | collective-permute-start | bytes 811016 | tf_op jit(solution)/shard_map/ppermute | solution.py:247
  10.4 26.9 %collective-permute-start.7 = (bf16[4,264,128]{2,1,0:T(8,128)(2,1)S(1)}, bf16[4,264,128]{2,1,0:T(8,128)(2,1)S(1)}, u32[]{:S(2)}, u32[]{:S(2)}) collective-permute-start(bf16[4,264,128]{2,1,0:T(8,128)(2,1)S(1)} %merge.1.refs_1_.refs_2_), channel_id=1, source_target_pairs={{0,4},{4,0},{1,5},{5,1},{2,6},{6,2},{3,7},{7,3},{8,12},{12,8},{9,1... | collective-permute-start | bytes 811016 | tf_op jit(solution)/shard_map/ppermute | solution.py:267
  17.9 20.5 %collective-permute-start.8 = (bf16[4,264,128]{2,1,0:T(8,128)(2,1)S(1)}, bf16[4,264,128]{2,1,0:T(8,128)(2,1)S(1)}, u32[]{:S(2)}, u32[]{:S(2)}) collective-permute-start(bf16[4,264,128]{2,1,0:T(8,128)(2,1)S(1)} %collective-permute-done.6.refs_3_), channel_id=1, source_target_pairs={{0,4},{4,0},{1,5},{5,1},{2,6},{6,2},{3,7},{7,3},{8,12},{12,8},{9,1... | collective-permute-start | bytes 811016 | tf_op jit(solution)/shard_map/ppermute | solution.py:267
  20.7 35.8 %collective-permute-start.11 = (bf16[4,264,128]{2,1,0:T(8,128)(2,1)S(1)}, bf16[4,264,128]{2,1,0:T(8,128)(2,1)S(1)}, u32[]{:S(2)}, u32[]{:S(2)}) collective-permute-start(bf16[4,264,128]{2,1,0:T(8,128)(2,1)S(1)} %collective-permute-done.9.refs_2_), channel_id=1, source_target_pairs={{0,4},{4,0},{1,5},{5,1},{2,6},{6,2},{3,7},{7,3},{8,12},{12,8},{9,1... | collective-permute-start | bytes 811016 | tf_op jit(solution)/shard_map/ppermute | solution.py:267
  32.5 24.1 %collective-permute-start.12 = (bf16[4,264,128]{2,1,0:T(8,128)(2,1)S(1)}, bf16[4,264,128]{2,1,0:T(8,128)(2,1)S(1)}, u32[]{:S(2)}, u32[]{:S(2)}) collective-permute-start(bf16[4,264,128]{2,1,0:T(8,128)(2,1)S(1)} %collective-permute-done.10.refs_3_), channel_id=1, source_target_pairs={{0,4},{4,0},{1,5},{5,1},{2,6},{6,2},{3,7},{7,3},{8,12},{12,8},{9,1... | collective-permute-start | bytes 811016 | tf_op jit(solution)/shard_map/ppermute | solution.py:267
  36.5 8.9 %collective-permute-start.2 = (bf16[128,1024]{1,0:T(8,128)(2,1)S(1)}, bf16[128,1024]{1,0:T(8,128)(2,1)S(1)}, u32[]{:S(2)}, u32[]{:S(2)}) collective-permute-start(bf16[128,1024]{1,0:T(8,128)(2,1)S(1)} %get-tuple-element.38), channel_id=1, source_target_pairs={{0,24},{8,16},{16,8},{24,0},{1,25},{9,17},{17,9},{25,1},{2,26},{10... | collective-permute-start | bytes 786440 | tf_op jit(solution)/shard_map/ppermute | solution.py:247
  37.2 13.7 %collective-permute-start.1 = (bf16[128,1024]{1,0:T(8,128)(2,1)S(1)}, bf16[128,1024]{1,0:T(8,128)(2,1)S(1)}, u32[]{:S(2)}, u32[]{:S(2)}) collective-permute-start(bf16[128,1024]{1,0:T(8,128)(2,1)S(1)} %get-tuple-element.37), channel_id=1, source_target_pairs={{0,16},{8,24},{16,0},{24,8},{1,17},{9,25},{17,1},{25,9},{2,18},{10... | collective-permute-start | bytes 786440 | tf_op jit(solution)/shard_map/ppermute | solution.py:247
  38.4 15.4 %collective-permute-start = (bf16[128,1024]{1,0:T(8,128)(2,1)S(1)}, bf16[128,1024]{1,0:T(8,128)(2,1)S(1)}, u32[]{:S(2)}, u32[]{:S(2)}) collective-permute-start(bf16[128,1024]{1,0:T(8,128)(2,1)S(1)} %get-tuple-element.36), channel_id=1, source_target_pairs={{0,8},{8,0},{16,24},{24,16},{1,9},{9,1},{17,25},{25,17},{2,10},{10... | collective-permute-start | bytes 786440 | tf_op jit(solution)/shard_map/ppermute | solution.py:247
  60.3 13.3 %collective-permute-start.15 = (bf16[128,1024]{1,0:T(8,128)(2,1)S(1)}, bf16[128,1024]{1,0:T(8,128)(2,1)S(1)}, u32[]{:S(2)}, u32[]{:S(2)}) collective-permute-start(bf16[128,1024]{1,0:T(8,128)(2,1)S(1)} %attend.15), channel_id=1, source_target_pairs={{0,16},{8,24},{16,0},{24,8},{1,17},{9,25},{17,1},{25,9},{2,18},{10... | collective-permute-start | bytes 786440 | tf_op jit(solution)/shard_map/ppermute | solution.py:247
  60.4 13.2 %collective-permute-start.14 = (bf16[128,1024]{1,0:T(8,128)(2,1)S(1)}, bf16[128,1024]{1,0:T(8,128)(2,1)S(1)}, u32[]{:S(2)}, u32[]{:S(2)}) collective-permute-start(bf16[128,1024]{1,0:T(8,128)(2,1)S(1)} %attend.14), channel_id=1, source_target_pairs={{0,24},{8,16},{16,8},{24,0},{1,25},{9,17},{17,9},{25,1},{2,26},{10... | collective-permute-start | bytes 786440 | tf_op jit(solution)/shard_map/ppermute | solution.py:247
  62.8 12.0 %collective-permute-start.13 = (bf16[128,1024]{1,0:T(8,128)(2,1)S(1)}, bf16[128,1024]{1,0:T(8,128)(2,1)S(1)}, u32[]{:S(2)}, u32[]{:S(2)}) collective-permute-start(bf16[128,1024]{1,0:T(8,128)(2,1)S(1)} %attend.16), channel_id=1, source_target_pairs={{0,8},{8,0},{16,24},{24,16},{1,9},{9,1},{17,25},{25,17},{2,10},{10... | collective-permute-start | bytes 786440 | tf_op jit(solution)/shard_map/ppermute | solution.py:247
where the time goes:
time: 75.7 us; the launch traced here: 75.6 us
  starting transfers between devices  29.3 us (39%)
  waiting for transfers between devices  26.5 us (35%)
  Pallas kernels  19.6 us (26%)
    ppermute x12, waiting for transfers between devices, swap(): return lax.ppermute(x, axis, [(g, g ^ i) for g in range(size)])  26.5 us
    ppermute x4, starting transfers between devices, local(): mate.append(lax.ppermute(own[j], 'core', [(0, 1), (1, 0)]))  18.4 us
    pallas_call x9, Pallas kernels, call(): pl.pallas_call(functools.partial(attend, index=i, turns=turns, **keep, **...  15.7 us
    ppermute x12, starting transfers between devices, swap(): return lax.ppermute(x, axis, [(g, g ^ i) for g in range(size)])  10.9 us
    pallas_call x2, Pallas kernels, put(): pl.pallas_call(functools.partial(place, turns=turns), out_shape=jax.Shape...  1.65 us
  transfers between devices with their start and end apart: 16, of which 9 were waited for; matrix products, arithmetic and copies ran while one was open for 0% of the time, Pallas kernels for 19%

commit v1 on v0

--- a/solution.py
+++ b/solution.py
@@ -191,14 +191,14 @@
             out_ref[:, h * HEAD_SIZE : (h + 1) * HEAD_SIZE] = (acc_ref[r, :] / total).astype(out_ref.dtype)
 
 
-def place(*refs, turns):
-    pieces, out_ref, sems = refs[: len(turns)], refs[-2], refs[-1]
+def place(*refs, groups):
+    pieces, out_ref, sems = refs[:groups], refs[groups], refs[groups + 1]
     width = pieces[0].shape[1]
     mine = lax.axis_index("group")
     copies = []
-    for i, piece in zip(turns, pieces):
+    for i in range(groups):
         start = pl.multiple_of((mine ^ i) * width, width)
-        copies.append(pltpu.make_async_copy(piece, out_ref.at[:, pl.ds(start, width)], sems.at[i]))
+        copies.append(pltpu.make_async_copy(pieces[i], out_ref.at[:, pl.ds(start, width)], sems.at[i]))
         copies[-1].start()
     for copy in copies:
         copy.wait()
@@ -267,7 +267,7 @@
         mate.append(lax.ppermute(own[j], "core", [(0, 1), (1, 0)]))
 
     held = [jax.ShapeDtypeStruct((per * rows, HEAD_SIZE), jnp.float32)] * 3
-    common = dict(rows=rows, groups=groups, layers=layers, split=2)
+    common = dict(rows=rows, groups=groups, layers=layers, split=1)
     units = 2 * (outer * groups // 2 + 1)
     near, far = list(range(layers // 2)), list(range(layers // 2, layers))
 
@@ -307,20 +307,15 @@
         follow(i)
         last = call(i, far, (False, True) if i == order[0] else both, states[i], True)
         out[i] = swap(last, "group", groups, i) if i else last
-
-    def put(turns, *rest):
-        return pl.pallas_call(
-            functools.partial(place, turns=turns),
-            out_shape=jax.ShapeDtypeStruct(queries.shape, jnp.bfloat16),
-            in_specs=[VMEM] * len(turns) + [HBM] * len(rest),
-            out_specs=HBM,
-            scratch_shapes=[pltpu.SemaphoreType.DMA((groups,))],
-            input_output_aliases={len(turns): 0} if rest else {},
-            compiler_params=limit(4),
-            name="place",
-        )(*(out[i] for i in turns), *rest)
-
-    return put(order[-1:], put([0] + order[:-1]))
+    return pl.pallas_call(
+        functools.partial(place, groups=groups),
+        out_shape=jax.ShapeDtypeStruct(queries.shape, jnp.bfloat16),
+        in_specs=[VMEM] * groups,
+        out_specs=HBM,
+        scratch_shapes=[pltpu.SemaphoreType.DMA((groups,))],
+        compiler_params=limit(4),
+        name="place",
+    )(*out)
 
 
 def solution(mesh):

time: 75.7 us -> 77.1 us (1.018)
  the two profiles are of different devices: /device:TPU:17 before, /device:TPU:0 now
where the time goes in v1:
time: 77.1 us; the launch traced here: 77 us
  waiting for transfers between devices  39.3 us (51%)
  Pallas kernels  20.9 us (27%)
  starting transfers between devices  16.6 us (22%)
    ppermute x12, waiting for transfers between devices, swap(): return lax.ppermute(x, axis, [(g, g ^ i) for g in range(size)])  39.3 us
    pallas_call x9, Pallas kernels, call(): pl.pallas_call(functools.partial(attend, index=i, turns=turns, **keep, **...  17.6 us
    ppermute x12, starting transfers between devices, swap(): return lax.ppermute(x, axis, [(g, g ^ i) for g in range(size)])  16.1 us
  transfers between devices with their start and end apart: 16, of which 9 were waited for; matrix products, arithmetic and copies ran while one was open for 0% of the time, Pallas kernels for 16%

profile of v1, /device:TPU:0, one launch (start us, length us, event | category | flops | bytes accessed | tf_op | source)
XLA Modules:
  0.0 77.0 jit_solution(17698876620754048561)
XLA Ops:
  0.0 1.1 %pack.1 = (bf16[264,128]{1,0:T(8,128)(2,1)S(1)}, bf16[264,128]{1,0:T(8,128)(2,1)S(1)}, bf16[264,128]{1,0:T(8,128)(2,1)S(1)}, bf16[264,128]{1,0:T(8,128)(2,1)S(1)}) custom-call(bf16[128,512]{1,0:T(8,128)(2,1)} %k_ref.1, bf16[128,512]{1,0:T(8,128)(2,1)} %v_ref.1, s32[1,128]{1,0:T(1,128)} %bitcast.1), custom_call_target="tpu_custom_call" | custom-call | tf_op jit(solution)/shard_map/pack/pallas_call | solution.py:219
  1.1 3.0 %collective-permute-start.3 = (bf16[264,128]{1,0:T(8,128)(2,1)S(1)}, bf16[264,128]{1,0:T(8,128)(2,1)S(1)}, u32[]{:S(2)}, u32[]{:S(2)}) collective-permute-start(bf16[264,128]{1,0:T(8,128)(2,1)S(1)} %get-tuple-element.41), channel_id=1, source_target_pairs={{0,8},{8,0},{16,24},{24,16},{1,9},{9,1},{17,25},{25,17},{2,10},{10... | collective-permute-start | bytes 202760 | tf_op jit(solution)/shard_map/ppermute | solution.py:247
  4.1 1.5 %collective-permute-start.4 = (bf16[264,128]{1,0:T(8,128)(2,1)S(1)}, bf16[264,128]{1,0:T(8,128)(2,1)S(1)}, u32[]{:S(2)}, u32[]{:S(2)}) collective-permute-start(bf16[264,128]{1,0:T(8,128)(2,1)S(1)} %get-tuple-element.42), channel_id=1, source_target_pairs={{0,16},{8,24},{16,0},{24,8},{1,17},{9,25},{17,1},{25,9},{2,18},{10... | collective-permute-start | bytes 202760 | tf_op jit(solution)/shard_map/ppermute | solution.py:247
  6.5 1.9 %collective-permute-done.4.refs_2_ = bf16[264,128]{1,0:T(8,128)(2,1)S(1)} collective-permute-done((bf16[264,128]{1,0:T(8,128)(2,1)S(1)}, bf16[264,128]{1,0:T(8,128)(2,1)S(1)}, u32[]{:S(2)}, u32[]{:S(2)}) %collective-permute-start.4) | collective-permute-done | bytes 67616 | tf_op jit(solution)/shard_map/ppermute | solution.py:247
  8.4 2.4 %collective-permute-done.5.refs_3_ = bf16[264,128]{1,0:T(8,128)(2,1)S(1)} collective-permute-done((bf16[264,128]{1,0:T(8,128)(2,1)S(1)}, bf16[264,128]{1,0:T(8,128)(2,1)S(1)}, u32[]{:S(2)}, u32[]{:S(2)}) %collective-permute-start.5) | collective-permute-done | bytes 67616 | tf_op jit(solution)/shard_map/ppermute | solution.py:247
  10.8 1.6 %collective-permute-start.6 = (bf16[4,264,128]{2,1,0:T(8,128)(2,1)S(1)}, bf16[4,264,128]{2,1,0:T(8,128)(2,1)S(1)}, u32[]{:S(2)}, u32[]{:S(2)}) collective-permute-start(bf16[4,264,128]{2,1,0:T(8,128)(2,1)S(1)} %merge.1.refs_1_.refs_2_), channel_id=1, source_target_pairs={{0,1},{1,0},{2,3},{3,2},{4,5},{5,4},{6,7},{7,6},{8,9},{9,8},{10,11... | collective-permute-start | bytes 811016 | tf_op jit(solution)/shard_map/ppermute | solution.py:247
  12.5 2.6 %collective-permute-start.9 = (bf16[4,264,128]{2,1,0:T(8,128)(2,1)S(1)}, bf16[4,264,128]{2,1,0:T(8,128)(2,1)S(1)}, u32[]{:S(2)}, u32[]{:S(2)}) collective-permute-start(bf16[4,264,128]{2,1,0:T(8,128)(2,1)S(1)} %merge.1.refs_1_.refs_2_), channel_id=1, source_target_pairs={{0,2},{1,3},{2,0},{3,1},{4,6},{5,7},{6,4},{7,5},{8,10},{9,11},{10,... | collective-permute-start | bytes 811016 | tf_op jit(solution)/shard_map/ppermute | solution.py:247
  15.3 6.1 %collective-permute-done.6.refs_3_ = bf16[4,264,128]{2,1,0:T(8,128)(2,1)S(1)} collective-permute-done((bf16[4,264,128]{2,1,0:T(8,128)(2,1)S(1)}, bf16[4,264,128]{2,1,0:T(8,128)(2,1)S(1)}, u32[]{:S(2)}, u32[]{:S(2)}) %collective-permute-start.6) | collective-permute-done | bytes 270368 | tf_op jit(solution)/shard_map/ppermute | solution.py:247
  21.4 12.7 %collective-permute-done.9.refs_2_ = bf16[4,264,128]{2,1,0:T(8,128)(2,1)S(1)} collective-permute-done((bf16[4,264,128]{2,1,0:T(8,128)(2,1)S(1)}, bf16[4,264,128]{2,1,0:T(8,128)(2,1)S(1)}, u32[]{:S(2)}, u32[]{:S(2)}) %collective-permute-start.9) | collective-permute-done | bytes 270368 | tf_op jit(solution)/shard_map/ppermute | solution.py:247
  34.7 1.2 %pack_queries.1 = (bf16[128,1024]{1,0:T(8,128)(2,1)S(1)}, bf16[128,1024]{1,0:T(8,128)(2,1)S(1)}, bf16[128,1024]{1,0:T(8,128)(2,1)S(1)}, bf16[128,1024]{1,0:T(8,128)(2,1)S(1)}) custom-call(bf16[128,4096]{1,0:T(8,128)(2,1)} %q_ref.1), custom_call_target="tpu_custom_call" | custom-call | tf_op jit(solution)/shard_map/pack_queries/pallas_call | solution.py:235
  36.6 1.5 %collective-permute-start.1 = (bf16[128,1024]{1,0:T(8,128)(2,1)S(1)}, bf16[128,1024]{1,0:T(8,128)(2,1)S(1)}, u32[]{:S(2)}, u32[]{:S(2)}) collective-permute-start(bf16[128,1024]{1,0:T(8,128)(2,1)S(1)} %get-tuple-element.38), channel_id=1, source_target_pairs={{0,16},{8,24},{16,0},{24,8},{1,17},{9,25},{17,1},{25,9},{2,18},{10... | collective-permute-start | bytes 786440 | tf_op jit(solution)/shard_map/ppermute | solution.py:247
  38.1 1.3 %collective-permute-start = (bf16[128,1024]{1,0:T(8,128)(2,1)S(1)}, bf16[128,1024]{1,0:T(8,128)(2,1)S(1)}, u32[]{:S(2)}, u32[]{:S(2)}) collective-permute-start(bf16[128,1024]{1,0:T(8,128)(2,1)S(1)} %get-tuple-element.37), channel_id=1, source_target_pairs={{0,8},{8,0},{16,24},{24,16},{1,9},{9,1},{17,25},{25,17},{2,10},{10... | collective-permute-start | bytes 786440 | tf_op jit(solution)/shard_map/ppermute | solution.py:247
  40.5 5.6 %collective-permute-done.2.refs_0_ = bf16[128,1024]{1,0:T(8,128)(2,1)S(1)} collective-permute-done((bf16[128,1024]{1,0:T(8,128)(2,1)S(1)}, bf16[128,1024]{1,0:T(8,128)(2,1)S(1)}, u32[]{:S(2)}, u32[]{:S(2)}) %collective-permute-start.2) | collective-permute-done | bytes 262176 | tf_op jit(solution)/shard_map/ppermute | solution.py:247
  46.1 3.5 %attend.10 = (f32[1024,128]{1,0:T(8,128)S(1)}, f32[1024,128]{1,0:T(8,128)S(1)}, f32[1024,128]{1,0:T(8,128)S(1)}) custom-call(bf16[128,1024]{1,0:T(8,128)(2,1)S(1)} %collective-permute-done.2.refs_0_, bf16[4,264,128]{2,1,0:T(8,128)(2,1)S(1)} %merge.1.refs_1_.refs_2_, bf16[4,264,128]{2,1,0:T(8,128)(2,1)S(1)} %merge.1.refs_1_.refs_2_, ...), custom_call_target="tpu_custom_call" | custom-call | tf_op jit(solution)/shard_map/attend/pallas_call | solution.py:280
  50.2 2.3 %attend.11 = (f32[1024,128]{1,0:T(8,128)S(1)}, f32[1024,128]{1,0:T(8,128)S(1)}, f32[1024,128]{1,0:T(8,128)S(1)}) custom-call(bf16[128,1024]{1,0:T(8,128)(2,1)S(1)} %collective-permute-done.1.refs_0_, bf16[4,264,128]{2,1,0:T(8,128)(2,1)S(1)} %merge.1.refs_1_.refs_2_, bf16[4,264,128]{2,1,0:T(8,128)(2,1)S(1)} %merge.1.refs_1_.refs_2_, ...), custom_call_target="tpu_custom_call" | custom-call | tf_op jit(solution)/shard_map/attend/pallas_call | solution.py:280
  53.5 2.3 %attend.13 = (f32[1024,128]{1,0:T(8,128)S(1)}, f32[1024,128]{1,0:T(8,128)S(1)}, f32[1024,128]{1,0:T(8,128)S(1)}) custom-call(bf16[128,1024]{1,0:T(8,128)(2,1)S(1)} %collective-permute-done.2.refs_0_, bf16[4,264,128]{2,1,0:T(8,128)(2,1)S(1)} %merge.1.refs_1_.refs_2_, bf16[4,264,128]{2,1,0:T(8,128)(2,1)S(1)} %collective-permute-done.9.refs_2_, ...), custom_call_target="tpu_custom_call" | custom-call | tf_op jit(solution)/shard_map/attend/pallas_call | solution.py:280
  55.8 1.9 %attend.14 = bf16[128,1024]{1,0:T(8,128)(2,1)S(1)} custom-call(bf16[128,1024]{1,0:T(8,128)(2,1)S(1)} %collective-permute-done.2.refs_0_, bf16[4,264,128]{2,1,0:T(8,128)(2,1)S(1)} %merge.1.refs_1_.refs_2_, bf16[4,264,128]{2,1,0:T(8,128)(2,1)S(1)} %collective-permute-done.11.refs_2_.refs_4_, bf16[4,264,128]{2,1,0:T(8,128)(2,1)S(1)} %collective-permute-done.12.refs_3_.refs_5_, ...), custom_call_target="tpu_custom_call" | custom-call | tf_op jit(solution)/shard_map/attend/pallas_call | solution.py:280
  57.7 2.5 %attend.15 = bf16[128,1024]{1,0:T(8,128)(2,1)S(1)} custom-call(bf16[128,1024]{1,0:T(8,128)(2,1)S(1)} %collective-permute-done.1.refs_0_, bf16[4,264,128]{2,1,0:T(8,128)(2,1)S(1)} %merge.1.refs_1_.refs_2_, bf16[4,264,128]{2,1,0:T(8,128)(2,1)S(1)} %collective-permute-done.9.refs_2_, bf16[4,264,128]{2,1,0:T(8,128)(2,1)S(1)} %collective-permute-done.10.refs_3_, ...), custom_call_target="tpu_custom_call" | custom-call | tf_op jit(solution)/shard_map/attend/pallas_call | solution.py:280
  60.2 1.9 %attend.16 = bf16[128,1024]{1,0:T(8,128)(2,1)S(1)} custom-call(bf16[128,1024]{1,0:T(8,128)(2,1)S(1)} %collective-permute-done.refs_0_, bf16[4,264,128]{2,1,0:T(8,128)(2,1)S(1)} %merge.1.refs_1_.refs_2_, bf16[4,264,128]{2,1,0:T(8,128)(2,1)S(1)} %collective-permute-done.9.refs_2_, bf16[4,264,128]{2,1,0:T(8,128)(2,1)S(1)} %collective-permute-done.10.refs_3_, ...), custom_call_target="tpu_custom_call" | custom-call | tf_op jit(solution)/shard_map/attend/pallas_call | solution.py:280
  62.1 1.9 %collective-permute-start.13 = (bf16[128,1024]{1,0:T(8,128)(2,1)S(1)}, bf16[128,1024]{1,0:T(8,128)(2,1)S(1)}, u32[]{:S(2)}, u32[]{:S(2)}) collective-permute-start(bf16[128,1024]{1,0:T(8,128)(2,1)S(1)} %attend.16), channel_id=1, source_target_pairs={{0,8},{8,0},{16,24},{24,16},{1,9},{9,1},{17,25},{25,17},{2,10},{10... | collective-permute-start | bytes 786440 | tf_op jit(solution)/shard_map/ppermute | solution.py:247
  64.0 1.6 %collective-permute-start.15 = (bf16[128,1024]{1,0:T(8,128)(2,1)S(1)}, bf16[128,1024]{1,0:T(8,128)(2,1)S(1)}, u32[]{:S(2)}, u32[]{:S(2)}) collective-permute-start(bf16[128,1024]{1,0:T(8,128)(2,1)S(1)} %attend.14), channel_id=1, source_target_pairs={{0,24},{8,16},{16,8},{24,0},{1,25},{9,17},{17,9},{25,1},{2,26},{10... | collective-permute-start | bytes 786440 | tf_op jit(solution)/shard_map/ppermute | solution.py:247
  65.6 1.2 %attend.17.refs_0_ = bf16[128,1024]{1,0:T(8,128)(2,1)S(1)} custom-call(bf16[128,1024]{1,0:T(8,128)(2,1)S(1)} %get-tuple-element.64.refs_0_, bf16[4,264,128]{2,1,0:T(8,128)(2,1)S(1)} %merge.1.refs_1_.refs_2_, bf16[4,264,128]{2,1,0:T(8,128)(2,1)S(1)} %collective-permute-done.9.refs_2_, bf16[4,264,128]{2,1,0:T(8,128)(2,1)S(1)} %collective-permute-done.10.refs_3_, ...), custom_call_target="tpu_custom_call" | custom-call | tf_op jit(solution)/shard_map/attend/pallas_call | solution.py:280
  66.9 4.5 %collective-permute-done.13.refs_1_ = bf16[128,1024]{1,0:T(8,128)(2,1)S(1)} collective-permute-done((bf16[128,1024]{1,0:T(8,128)(2,1)S(1)}, bf16[128,1024]{1,0:T(8,128)(2,1)S(1)}, u32[]{:S(2)}, u32[]{:S(2)}) %collective-permute-start.13) | collective-permute-done | bytes 262176 | tf_op jit(solution)/shard_map/ppermute | solution.py:247
  71.3 4.7 %collective-permute-done.14.refs_2_ = bf16[128,1024]{1,0:T(8,128)(2,1)S(1)} collective-permute-done((bf16[128,1024]{1,0:T(8,128)(2,1)S(1)}, bf16[128,1024]{1,0:T(8,128)(2,1)S(1)}, u32[]{:S(2)}, u32[]{:S(2)}) %collective-permute-start.14) | collective-permute-done | bytes 262176 | tf_op jit(solution)/shard_map/ppermute | solution.py:247
  (21 shorter events, 6.0 us)
Async XLA Ops:
  1.1 5.4 %collective-permute-start.3 = (bf16[264,128]{1,0:T(8,128)(2,1)S(1)}, bf16[264,128]{1,0:T(8,128)(2,1)S(1)}, u32[]{:S(2)}, u32[]{:S(2)}) collective-permute-start(bf16[264,128]{1,0:T(8,128)(2,1)S(1)} %get-tuple-element.41), channel_id=1, source_target_pairs={{0,8},{8,0},{16,24},{24,16},{1,9},{9,1},{17,25},{25,17},{2,10},{10... | collective-permute-start | bytes 202760 | tf_op jit(solution)/shard_map/ppermute | solution.py:247
  4.1 4.3 %collective-permute-start.4 = (bf16[264,128]{1,0:T(8,128)(2,1)S(1)}, bf16[264,128]{1,0:T(8,128)(2,1)S(1)}, u32[]{:S(2)}, u32[]{:S(2)}) collective-permute-start(bf16[264,128]{1,0:T(8,128)(2,1)S(1)} %get-tuple-element.42), channel_id=1, source_target_pairs={{0,16},{8,24},{16,0},{24,8},{1,17},{9,25},{17,1},{25,9},{2,18},{10... | collective-permute-start | bytes 202760 | tf_op jit(solution)/shard_map/ppermute | solution.py:247
  5.6 5.2 %collective-permute-start.5 = (bf16[264,128]{1,0:T(8,128)(2,1)S(1)}, bf16[264,128]{1,0:T(8,128)(2,1)S(1)}, u32[]{:S(2)}, u32[]{:S(2)}) collective-permute-start(bf16[264,128]{1,0:T(8,128)(2,1)S(1)} %get-tuple-element.43), channel_id=1, source_target_pairs={{0,24},{8,16},{16,8},{24,0},{1,25},{9,17},{17,9},{25,1},{2,26},{10... | collective-permute-start | bytes 202760 | tf_op jit(solution)/shard_map/ppermute | solution.py:247
  10.8 10.6 %collective-permute-start.6 = (bf16[4,264,128]{2,1,0:T(8,128)(2,1)S(1)}, bf16[4,264,128]{2,1,0:T(8,128)(2,1)S(1)}, u32[]{:S(2)}, u32[]{:S(2)}) collective-permute-start(bf16[4,264,128]{2,1,0:T(8,128)(2,1)S(1)} %merge.1.refs_1_.refs_2_), channel_id=1, source_target_pairs={{0,1},{1,0},{2,3},{3,2},{4,5},{5,4},{6,7},{7,6},{8,9},{9,8},{10,11... | collective-permute-start | bytes 811016 | tf_op jit(solution)/shard_map/ppermute | solution.py:247
  12.5 21.7 %collective-permute-start.9 = (bf16[4,264,128]{2,1,0:T(8,128)(2,1)S(1)}, bf16[4,264,128]{2,1,0:T(8,128)(2,1)S(1)}, u32[]{:S(2)}, u32[]{:S(2)}) collective-permute-start(bf16[4,264,128]{2,1,0:T(8,128)(2,1)S(1)} %merge.1.refs_1_.refs_2_), channel_id=1, source_target_pairs={{0,2},{1,3},{2,0},{3,1},{4,6},{5,7},{6,4},{7,5},{8,10},{9,11},{10,... | collective-permute-start | bytes 811016 | tf_op jit(solution)/shard_map/ppermute | solution.py:247
  15.1 19.1 %collective-permute-start.10 = (bf16[4,264,128]{2,1,0:T(8,128)(2,1)S(1)}, bf16[4,264,128]{2,1,0:T(8,128)(2,1)S(1)}, u32[]{:S(2)}, u32[]{:S(2)}) collective-permute-start(bf16[4,264,128]{2,1,0:T(8,128)(2,1)S(1)} %merge.1.refs_1_.refs_2_), channel_id=1, source_target_pairs={{0,3},{1,2},{2,1},{3,0},{4,7},{5,6},{6,5},{7,4},{8,11},{9,10},{10,... | collective-permute-start | bytes 811016 | tf_op jit(solution)/shard_map/ppermute | solution.py:247
  15.3 21.3 %collective-permute-start.7 = (bf16[4,264,128]{2,1,0:T(8,128)(2,1)S(1)}, bf16[4,264,128]{2,1,0:T(8,128)(2,1)S(1)}, u32[]{:S(2)}, u32[]{:S(2)}) collective-permute-start(bf16[4,264,128]{2,1,0:T(8,128)(2,1)S(1)} %merge.1.refs_1_.refs_2_), channel_id=1, source_target_pairs={{0,4},{4,0},{1,5},{5,1},{2,6},{6,2},{3,7},{7,3},{8,12},{12,8},{9,1... | collective-permute-start | bytes 811016 | tf_op jit(solution)/shard_map/ppermute | solution.py:267
  21.4 16.7 %collective-permute-start.8 = (bf16[4,264,128]{2,1,0:T(8,128)(2,1)S(1)}, bf16[4,264,128]{2,1,0:T(8,128)(2,1)S(1)}, u32[]{:S(2)}, u32[]{:S(2)}) collective-permute-start(bf16[4,264,128]{2,1,0:T(8,128)(2,1)S(1)} %collective-permute-done.6.refs_3_), channel_id=1, source_target_pairs={{0,4},{4,0},{1,5},{5,1},{2,6},{6,2},{3,7},{7,3},{8,12},{12,8},{9,1... | collective-permute-start | bytes 811016 | tf_op jit(solution)/shard_map/ppermute | solution.py:267
  34.1 21.7 %collective-permute-start.11 = (bf16[4,264,128]{2,1,0:T(8,128)(2,1)S(1)}, bf16[4,264,128]{2,1,0:T(8,128)(2,1)S(1)}, u32[]{:S(2)}, u32[]{:S(2)}) collective-permute-start(bf16[4,264,128]{2,1,0:T(8,128)(2,1)S(1)} %collective-permute-done.9.refs_2_), channel_id=1, source_target_pairs={{0,4},{4,0},{1,5},{5,1},{2,6},{6,2},{3,7},{7,3},{8,12},{12,8},{9,1... | collective-permute-start | bytes 811016 | tf_op jit(solution)/shard_map/ppermute | solution.py:267
  34.1 21.7 %collective-permute-start.12 = (bf16[4,264,128]{2,1,0:T(8,128)(2,1)S(1)}, bf16[4,264,128]{2,1,0:T(8,128)(2,1)S(1)}, u32[]{:S(2)}, u32[]{:S(2)}) collective-permute-start(bf16[4,264,128]{2,1,0:T(8,128)(2,1)S(1)} %collective-permute-done.10.refs_3_), channel_id=1, source_target_pairs={{0,4},{4,0},{1,5},{5,1},{2,6},{6,2},{3,7},{7,3},{8,12},{12,8},{9,1... | collective-permute-start | bytes 811016 | tf_op jit(solution)/shard_map/ppermute | solution.py:267
  35.9 10.2 %collective-permute-start.2 = (bf16[128,1024]{1,0:T(8,128)(2,1)S(1)}, bf16[128,1024]{1,0:T(8,128)(2,1)S(1)}, u32[]{:S(2)}, u32[]{:S(2)}) collective-permute-start(bf16[128,1024]{1,0:T(8,128)(2,1)S(1)} %get-tuple-element.39), channel_id=1, source_target_pairs={{0,24},{8,16},{16,8},{24,0},{1,25},{9,17},{17,9},{25,1},{2,26},{10... | collective-permute-start | bytes 786440 | tf_op jit(solution)/shard_map/ppermute | solution.py:247
  36.6 13.6 %collective-permute-start.1 = (bf16[128,1024]{1,0:T(8,128)(2,1)S(1)}, bf16[128,1024]{1,0:T(8,128)(2,1)S(1)}, u32[]{:S(2)}, u32[]{:S(2)}) collective-permute-start(bf16[128,1024]{1,0:T(8,128)(2,1)S(1)} %get-tuple-element.38), channel_id=1, source_target_pairs={{0,16},{8,24},{16,0},{24,8},{1,17},{9,25},{17,1},{25,9},{2,18},{10... | collective-permute-start | bytes 786440 | tf_op jit(solution)/shard_map/ppermute | solution.py:247
  38.1 14.3 %collective-permute-start = (bf16[128,1024]{1,0:T(8,128)(2,1)S(1)}, bf16[128,1024]{1,0:T(8,128)(2,1)S(1)}, u32[]{:S(2)}, u32[]{:S(2)}) collective-permute-start(bf16[128,1024]{1,0:T(8,128)(2,1)S(1)} %get-tuple-element.37), channel_id=1, source_target_pairs={{0,8},{8,0},{16,24},{24,16},{1,9},{9,1},{17,25},{25,17},{2,10},{10... | collective-permute-start | bytes 786440 | tf_op jit(solution)/shard_map/ppermute | solution.py:247
  62.1 9.2 %collective-permute-start.13 = (bf16[128,1024]{1,0:T(8,128)(2,1)S(1)}, bf16[128,1024]{1,0:T(8,128)(2,1)S(1)}, u32[]{:S(2)}, u32[]{:S(2)}) collective-permute-start(bf16[128,1024]{1,0:T(8,128)(2,1)S(1)} %attend.16), channel_id=1, source_target_pairs={{0,8},{8,0},{16,24},{24,16},{1,9},{9,1},{17,25},{25,17},{2,10},{10... | collective-permute-start | bytes 786440 | tf_op jit(solution)/shard_map/ppermute | solution.py:247
  64.0 12.0 %collective-permute-start.14 = (bf16[128,1024]{1,0:T(8,128)(2,1)S(1)}, bf16[128,1024]{1,0:T(8,128)(2,1)S(1)}, u32[]{:S(2)}, u32[]{:S(2)}) collective-permute-start(bf16[128,1024]{1,0:T(8,128)(2,1)S(1)} %attend.15), channel_id=1, source_target_pairs={{0,16},{8,24},{16,0},{24,8},{1,17},{9,25},{17,1},{25,9},{2,18},{10... | collective-permute-start | bytes 786440 | tf_op jit(solution)/shard_map/ppermute | solution.py:247
  64.0 12.0 %collective-permute-start.15 = (bf16[128,1024]{1,0:T(8,128)(2,1)S(1)}, bf16[128,1024]{1,0:T(8,128)(2,1)S(1)}, u32[]{:S(2)}, u32[]{:S(2)}) collective-permute-start(bf16[128,1024]{1,0:T(8,128)(2,1)S(1)} %attend.14), channel_id=1, source_target_pairs={{0,24},{8,16},{16,8},{24,0},{1,25},{9,17},{17,9},{25,1},{2,26},{10... | collective-permute-start | bytes 786440 | tf_op jit(solution)/shard_map/ppermute | solution.py:247

commit v2 on v1

--- a/solution.py
+++ b/solution.py
@@ -104,10 +104,11 @@
     m_ref[...] = jnp.full(m_ref.shape, LOW, jnp.float32)
     part = per // split
     heads = list(range(per))
-    last_own, last_mate = home + 1, home + core
+    earlier = functools.reduce(jnp.logical_or, [(layer ^ turn) <= layer for turn in turns])
+    last_own, last_mate = home + jnp.where(earlier, 1, 0), home + core
     first_own = skipped(own) if own else last_own
     first_mate = skipped(mate) if mate else last_mate
-    second = last_own - first_own
+    second = jnp.maximum(last_own - first_own, 0)
 
     def strip(h):
         return pl.ds(h * rows, rows)
@@ -267,7 +268,7 @@
         mate.append(lax.ppermute(own[j], "core", [(0, 1), (1, 0)]))
 
     held = [jax.ShapeDtypeStruct((per * rows, HEAD_SIZE), jnp.float32)] * 3
-    common = dict(rows=rows, groups=groups, layers=layers, split=1)
+    common = dict(rows=rows, groups=groups, layers=layers, split=2)
     units = 2 * (outer * groups // 2 + 1)
     near, far = list(range(layers // 2)), list(range(layers // 2, layers))
 

time: 77.1 us -> 76.2 us (0.988)
  the two profiles are of different devices: /device:TPU:0 before, /device:TPU:19 now
where the time goes in v2:
time: 76.2 us; the launch traced here: 76.1 us
  starting transfers between devices  30.1 us (40%)
  waiting for transfers between devices  26.9 us (35%)
  Pallas kernels  19 us (25%)
    ppermute x12, waiting for transfers between devices, swap(): return lax.ppermute(x, axis, [(g, g ^ i) for g in range(size)])  26.9 us
    ppermute x4, starting transfers between devices, local(): mate.append(lax.ppermute(own[j], 'core', [(0, 1), (1, 0)]))  17.6 us
    pallas_call x9, Pallas kernels, call(): pl.pallas_call(functools.partial(attend, index=i, turns=turns, **keep, **...  15.7 us
    ppermute x12, starting transfers between devices, swap(): return lax.ppermute(x, axis, [(g, g ^ i) for g in range(size)])  12.5 us
  transfers between devices with their start and end apart: 16, of which 9 were waited for; matrix products, arithmetic and copies ran while one was open for 0% of the time, Pallas kernels for 16%

profile of v2, /device:TPU:19, one launch (start us, length us, event | category | flops | bytes accessed | tf_op | source)
XLA Modules:
  0.0 76.1 jit_solution(950742879648490955)
XLA Ops:
  1.4 1.2 %collective-permute-start.4 = (bf16[264,128]{1,0:T(8,128)(2,1)S(1)}, bf16[264,128]{1,0:T(8,128)(2,1)S(1)}, u32[]{:S(2)}, u32[]{:S(2)}) collective-permute-start(bf16[264,128]{1,0:T(8,128)(2,1)S(1)} %get-tuple-element.42), channel_id=1, source_target_pairs={{0,16},{8,24},{16,0},{24,8},{1,17},{9,25},{17,1},{25,9},{2,18},{10... | collective-permute-start | bytes 202760 | tf_op jit(solution)/shard_map/ppermute | solution.py:248
  4.5 2.6 %collective-permute-done.5.refs_3_ = bf16[264,128]{1,0:T(8,128)(2,1)S(1)} collective-permute-done((bf16[264,128]{1,0:T(8,128)(2,1)S(1)}, bf16[264,128]{1,0:T(8,128)(2,1)S(1)}, u32[]{:S(2)}, u32[]{:S(2)}) %collective-permute-start.5) | collective-permute-done | bytes 67616 | tf_op jit(solution)/shard_map/ppermute | solution.py:248
  7.1 1.4 %collective-permute-start.6 = (bf16[4,264,128]{2,1,0:T(8,128)(2,1)S(1)}, bf16[4,264,128]{2,1,0:T(8,128)(2,1)S(1)}, u32[]{:S(2)}, u32[]{:S(2)}) collective-permute-start(bf16[4,264,128]{2,1,0:T(8,128)(2,1)S(1)} %merge.1.refs_1_.refs_2_), channel_id=1, source_target_pairs={{0,1},{1,0},{2,3},{3,2},{4,5},{5,4},{6,7},{7,6},{8,9},{9,8},{10,11... | collective-permute-start | bytes 811016 | tf_op jit(solution)/shard_map/ppermute | solution.py:248
  8.5 1.3 %collective-permute-start.10 = (bf16[4,264,128]{2,1,0:T(8,128)(2,1)S(1)}, bf16[4,264,128]{2,1,0:T(8,128)(2,1)S(1)}, u32[]{:S(2)}, u32[]{:S(2)}) collective-permute-start(bf16[4,264,128]{2,1,0:T(8,128)(2,1)S(1)} %merge.1.refs_1_.refs_2_), channel_id=1, source_target_pairs={{0,3},{1,2},{2,1},{3,0},{4,7},{5,6},{6,5},{7,4},{8,11},{9,10},{10,... | collective-permute-start | bytes 811016 | tf_op jit(solution)/shard_map/ppermute | solution.py:248
  9.8 2.8 %collective-permute-start.7 = (bf16[4,264,128]{2,1,0:T(8,128)(2,1)S(1)}, bf16[4,264,128]{2,1,0:T(8,128)(2,1)S(1)}, u32[]{:S(2)}, u32[]{:S(2)}) collective-permute-start(bf16[4,264,128]{2,1,0:T(8,128)(2,1)S(1)} %merge.1.refs_1_.refs_2_), channel_id=1, source_target_pairs={{0,4},{4,0},{1,5},{5,1},{2,6},{6,2},{3,7},{7,3},{8,12},{12,8},{9,1... | collective-permute-start | bytes 811016 | tf_op jit(solution)/shard_map/ppermute | solution.py:268
  12.6 4.8 %collective-permute-done.6.refs_3_ = bf16[4,264,128]{2,1,0:T(8,128)(2,1)S(1)} collective-permute-done((bf16[4,264,128]{2,1,0:T(8,128)(2,1)S(1)}, bf16[4,264,128]{2,1,0:T(8,128)(2,1)S(1)}, u32[]{:S(2)}, u32[]{:S(2)}) %collective-permute-start.6) | collective-permute-done | bytes 270368 | tf_op jit(solution)/shard_map/ppermute | solution.py:248
  17.5 2.3 %collective-permute-start.8 = (bf16[4,264,128]{2,1,0:T(8,128)(2,1)S(1)}, bf16[4,264,128]{2,1,0:T(8,128)(2,1)S(1)}, u32[]{:S(2)}, u32[]{:S(2)}) collective-permute-start(bf16[4,264,128]{2,1,0:T(8,128)(2,1)S(1)} %collective-permute-done.6.refs_3_), channel_id=1, source_target_pairs={{0,4},{4,0},{1,5},{5,1},{2,6},{6,2},{3,7},{7,3},{8,12},{12,8},{9,1... | collective-permute-start | bytes 811016 | tf_op jit(solution)/shard_map/ppermute | solution.py:268
  19.8 9.7 %collective-permute-start.11 = (bf16[4,264,128]{2,1,0:T(8,128)(2,1)S(1)}, bf16[4,264,128]{2,1,0:T(8,128)(2,1)S(1)}, u32[]{:S(2)}, u32[]{:S(2)}) collective-permute-start(bf16[4,264,128]{2,1,0:T(8,128)(2,1)S(1)} %collective-permute-done.9.refs_2_), channel_id=1, source_target_pairs={{0,4},{4,0},{1,5},{5,1},{2,6},{6,2},{3,7},{7,3},{8,12},{12,8},{9,1... | collective-permute-start | bytes 811016 | tf_op jit(solution)/shard_map/ppermute | solution.py:268
  29.5 2.4 %collective-permute-done.10.refs_3_ = bf16[4,264,128]{2,1,0:T(8,128)(2,1)S(1)} collective-permute-done((bf16[4,264,128]{2,1,0:T(8,128)(2,1)S(1)}, bf16[4,264,128]{2,1,0:T(8,128)(2,1)S(1)}, u32[]{:S(2)}, u32[]{:S(2)}) %collective-permute-start.10) | collective-permute-done | bytes 270368 | tf_op jit(solution)/shard_map/ppermute | solution.py:248
  31.9 2.7 %collective-permute-start.12 = (bf16[4,264,128]{2,1,0:T(8,128)(2,1)S(1)}, bf16[4,264,128]{2,1,0:T(8,128)(2,1)S(1)}, u32[]{:S(2)}, u32[]{:S(2)}) collective-permute-start(bf16[4,264,128]{2,1,0:T(8,128)(2,1)S(1)} %collective-permute-done.10.refs_3_), channel_id=1, source_target_pairs={{0,4},{4,0},{1,5},{5,1},{2,6},{6,2},{3,7},{7,3},{8,12},{12,8},{9,1... | collective-permute-start | bytes 811016 | tf_op jit(solution)/shard_map/ppermute | solution.py:268
  34.7 1.2 %pack_queries.1 = (bf16[128,1024]{1,0:T(8,128)(2,1)S(1)}, bf16[128,1024]{1,0:T(8,128)(2,1)S(1)}, bf16[128,1024]{1,0:T(8,128)(2,1)S(1)}, bf16[128,1024]{1,0:T(8,128)(2,1)S(1)}) custom-call(bf16[128,4096]{1,0:T(8,128)(2,1)} %q_ref.1), custom_call_target="tpu_custom_call" | custom-call | tf_op jit(solution)/shard_map/pack_queries/pallas_call | solution.py:236
  38.6 1.6 %attend.9 = (f32[1024,128]{1,0:T(8,128)S(1)}, f32[1024,128]{1,0:T(8,128)S(1)}, f32[1024,128]{1,0:T(8,128)S(1)}) custom-call(bf16[128,1024]{1,0:T(8,128)(2,1)S(1)} %get-tuple-element.64.refs_0_, bf16[4,264,128]{2,1,0:T(8,128)(2,1)S(1)} %merge.1.refs_1_.refs_2_, bf16[4,264,128]{2,1,0:T(8,128)(2,1)S(1)} %merge.1.refs_1_.refs_2_, ...), custom_call_target="tpu_custom_call" | custom-call | tf_op jit(solution)/shard_map/attend/pallas_call | solution.py:281
  40.3 4.5 %collective-permute-done.2.refs_0_ = bf16[128,1024]{1,0:T(8,128)(2,1)S(1)} collective-permute-done((bf16[128,1024]{1,0:T(8,128)(2,1)S(1)}, bf16[128,1024]{1,0:T(8,128)(2,1)S(1)}, u32[]{:S(2)}, u32[]{:S(2)}) %collective-permute-start.2) | collective-permute-done | bytes 262176 | tf_op jit(solution)/shard_map/ppermute | solution.py:248
  44.8 2.9 %attend.10 = (f32[1024,128]{1,0:T(8,128)S(1)}, f32[1024,128]{1,0:T(8,128)S(1)}, f32[1024,128]{1,0:T(8,128)S(1)}) custom-call(bf16[128,1024]{1,0:T(8,128)(2,1)S(1)} %collective-permute-done.2.refs_0_, bf16[4,264,128]{2,1,0:T(8,128)(2,1)S(1)} %merge.1.refs_1_.refs_2_, bf16[4,264,128]{2,1,0:T(8,128)(2,1)S(1)} %merge.1.refs_1_.refs_2_, ...), custom_call_target="tpu_custom_call" | custom-call | tf_op jit(solution)/shard_map/attend/pallas_call | solution.py:281
  47.7 2.8 %collective-permute-done.1.refs_0_ = bf16[128,1024]{1,0:T(8,128)(2,1)S(1)} collective-permute-done((bf16[128,1024]{1,0:T(8,128)(2,1)S(1)}, bf16[128,1024]{1,0:T(8,128)(2,1)S(1)}, u32[]{:S(2)}, u32[]{:S(2)}) %collective-permute-start.1) | collective-permute-done | bytes 262176 | tf_op jit(solution)/shard_map/ppermute | solution.py:248
  51.5 1.6 %attend.12 = (f32[1024,128]{1,0:T(8,128)S(1)}, f32[1024,128]{1,0:T(8,128)S(1)}, f32[1024,128]{1,0:T(8,128)S(1)}) custom-call(bf16[128,1024]{1,0:T(8,128)(2,1)S(1)} %collective-permute-done.refs_0_, bf16[4,264,128]{2,1,0:T(8,128)(2,1)S(1)} %merge.1.refs_1_.refs_2_, bf16[4,264,128]{2,1,0:T(8,128)(2,1)S(1)} %merge.1.refs_1_.refs_2_, ...), custom_call_target="tpu_custom_call" | custom-call | tf_op jit(solution)/shard_map/attend/pallas_call | solution.py:281
  53.2 1.7 %attend.13 = (f32[1024,128]{1,0:T(8,128)S(1)}, f32[1024,128]{1,0:T(8,128)S(1)}, f32[1024,128]{1,0:T(8,128)S(1)}) custom-call(bf16[128,1024]{1,0:T(8,128)(2,1)S(1)} %collective-permute-done.2.refs_0_, bf16[4,264,128]{2,1,0:T(8,128)(2,1)S(1)} %merge.1.refs_1_.refs_2_, bf16[4,264,128]{2,1,0:T(8,128)(2,1)S(1)} %collective-permute-done.9.refs_2_, ...), custom_call_target="tpu_custom_call" | custom-call | tf_op jit(solution)/shard_map/attend/pallas_call | solution.py:281
  54.9 1.9 %attend.14 = bf16[128,1024]{1,0:T(8,128)(2,1)S(1)} custom-call(bf16[128,1024]{1,0:T(8,128)(2,1)S(1)} %collective-permute-done.2.refs_0_, bf16[4,264,128]{2,1,0:T(8,128)(2,1)S(1)} %merge.1.refs_1_.refs_2_, bf16[4,264,128]{2,1,0:T(8,128)(2,1)S(1)} %collective-permute-done.11.refs_2_.refs_4_, bf16[4,264,128]{2,1,0:T(8,128)(2,1)S(1)} %collective-permute-done.12.refs_3_.refs_5_, ...), custom_call_target="tpu_custom_call" | custom-call | tf_op jit(solution)/shard_map/attend/pallas_call | solution.py:281
  56.8 1.2 %attend.15 = bf16[128,1024]{1,0:T(8,128)(2,1)S(1)} custom-call(bf16[128,1024]{1,0:T(8,128)(2,1)S(1)} %collective-permute-done.1.refs_0_, bf16[4,264,128]{2,1,0:T(8,128)(2,1)S(1)} %merge.1.refs_1_.refs_2_, bf16[4,264,128]{2,1,0:T(8,128)(2,1)S(1)} %collective-permute-done.9.refs_2_, bf16[4,264,128]{2,1,0:T(8,128)(2,1)S(1)} %collective-permute-done.10.refs_3_, ...), custom_call_target="tpu_custom_call" | custom-call | tf_op jit(solution)/shard_map/attend/pallas_call | solution.py:281
  58.0 1.9 %attend.16 = bf16[128,1024]{1,0:T(8,128)(2,1)S(1)} custom-call(bf16[128,1024]{1,0:T(8,128)(2,1)S(1)} %collective-permute-done.refs_0_, bf16[4,264,128]{2,1,0:T(8,128)(2,1)S(1)} %merge.1.refs_1_.refs_2_, bf16[4,264,128]{2,1,0:T(8,128)(2,1)S(1)} %collective-permute-done.9.refs_2_, bf16[4,264,128]{2,1,0:T(8,128)(2,1)S(1)} %collective-permute-done.10.refs_3_, ...), custom_call_target="tpu_custom_call" | custom-call | tf_op jit(solution)/shard_map/attend/pallas_call | solution.py:281
  59.9 2.6 %collective-permute-start.13 = (bf16[128,1024]{1,0:T(8,128)(2,1)S(1)}, bf16[128,1024]{1,0:T(8,128)(2,1)S(1)}, u32[]{:S(2)}, u32[]{:S(2)}) collective-permute-start(bf16[128,1024]{1,0:T(8,128)(2,1)S(1)} %attend.16), channel_id=1, source_target_pairs={{0,8},{8,0},{16,24},{24,16},{1,9},{9,1},{17,25},{25,17},{2,10},{10... | collective-permute-start | bytes 786440 | tf_op jit(solution)/shard_map/ppermute | solution.py:248
  64.2 1.8 %attend.17.refs_0_ = bf16[128,1024]{1,0:T(8,128)(2,1)S(1)} custom-call(bf16[128,1024]{1,0:T(8,128)(2,1)S(1)} %get-tuple-element.64.refs_0_, bf16[4,264,128]{2,1,0:T(8,128)(2,1)S(1)} %merge.1.refs_1_.refs_2_, bf16[4,264,128]{2,1,0:T(8,128)(2,1)S(1)} %collective-permute-done.9.refs_2_, bf16[4,264,128]{2,1,0:T(8,128)(2,1)S(1)} %collective-permute-done.10.refs_3_, ...), custom_call_target="tpu_custom_call" | custom-call | tf_op jit(solution)/shard_map/attend/pallas_call | solution.py:281
  66.1 3.3 %collective-permute-done.13.refs_1_ = bf16[128,1024]{1,0:T(8,128)(2,1)S(1)} collective-permute-done((bf16[128,1024]{1,0:T(8,128)(2,1)S(1)}, bf16[128,1024]{1,0:T(8,128)(2,1)S(1)}, u32[]{:S(2)}, u32[]{:S(2)}) %collective-permute-start.13) | collective-permute-done | bytes 262176 | tf_op jit(solution)/shard_map/ppermute | solution.py:248
  69.4 5.7 %collective-permute-done.14.refs_2_ = bf16[128,1024]{1,0:T(8,128)(2,1)S(1)} collective-permute-done((bf16[128,1024]{1,0:T(8,128)(2,1)S(1)}, bf16[128,1024]{1,0:T(8,128)(2,1)S(1)}, u32[]{:S(2)}, u32[]{:S(2)}) %collective-permute-start.14) | collective-permute-done | bytes 262176 | tf_op jit(solution)/shard_map/ppermute | solution.py:248
  (21 shorter events, 9.8 us)
Async XLA Ops:
  1.1 3.2 %collective-permute-start.3 = (bf16[264,128]{1,0:T(8,128)(2,1)S(1)}, bf16[264,128]{1,0:T(8,128)(2,1)S(1)}, u32[]{:S(2)}, u32[]{:S(2)}) collective-permute-start(bf16[264,128]{1,0:T(8,128)(2,1)S(1)} %get-tuple-element.41), channel_id=1, source_target_pairs={{0,8},{8,0},{16,24},{24,16},{1,9},{9,1},{17,25},{25,17},{2,10},{10... | collective-permute-start | bytes 202760 | tf_op jit(solution)/shard_map/ppermute | solution.py:248
  1.4 3.1 %collective-permute-start.4 = (bf16[264,128]{1,0:T(8,128)(2,1)S(1)}, bf16[264,128]{1,0:T(8,128)(2,1)S(1)}, u32[]{:S(2)}, u32[]{:S(2)}) collective-permute-start(bf16[264,128]{1,0:T(8,128)(2,1)S(1)} %get-tuple-element.42), channel_id=1, source_target_pairs={{0,16},{8,24},{16,0},{24,8},{1,17},{9,25},{17,1},{25,9},{2,18},{10... | collective-permute-start | bytes 202760 | tf_op jit(solution)/shard_map/ppermute | solution.py:248
  2.6 4.5 %collective-permute-start.5 = (bf16[264,128]{1,0:T(8,128)(2,1)S(1)}, bf16[264,128]{1,0:T(8,128)(2,1)S(1)}, u32[]{:S(2)}, u32[]{:S(2)}) collective-permute-start(bf16[264,128]{1,0:T(8,128)(2,1)S(1)} %get-tuple-element.43), channel_id=1, source_target_pairs={{0,24},{8,16},{16,8},{24,0},{1,25},{9,17},{17,9},{25,1},{2,26},{10... | collective-permute-start | bytes 202760 | tf_op jit(solution)/shard_map/ppermute | solution.py:248
  7.1 10.4 %collective-permute-start.6 = (bf16[4,264,128]{2,1,0:T(8,128)(2,1)S(1)}, bf16[4,264,128]{2,1,0:T(8,128)(2,1)S(1)}, u32[]{:S(2)}, u32[]{:S(2)}) collective-permute-start(bf16[4,264,128]{2,1,0:T(8,128)(2,1)S(1)} %merge.1.refs_1_.refs_2_), channel_id=1, source_target_pairs={{0,1},{1,0},{2,3},{3,2},{4,5},{5,4},{6,7},{7,6},{8,9},{9,8},{10,11... | collective-permute-start | bytes 811016 | tf_op jit(solution)/shard_map/ppermute | solution.py:248
  8.5 11.3 %collective-permute-start.9 = (bf16[4,264,128]{2,1,0:T(8,128)(2,1)S(1)}, bf16[4,264,128]{2,1,0:T(8,128)(2,1)S(1)}, u32[]{:S(2)}, u32[]{:S(2)}) collective-permute-start(bf16[4,264,128]{2,1,0:T(8,128)(2,1)S(1)} %merge.1.refs_1_.refs_2_), channel_id=1, source_target_pairs={{0,2},{1,3},{2,0},{3,1},{4,6},{5,7},{6,4},{7,5},{8,10},{9,11},{10,... | collective-permute-start | bytes 811016 | tf_op jit(solution)/shard_map/ppermute | solution.py:248
  8.5 23.4 %collective-permute-start.10 = (bf16[4,264,128]{2,1,0:T(8,128)(2,1)S(1)}, bf16[4,264,128]{2,1,0:T(8,128)(2,1)S(1)}, u32[]{:S(2)}, u32[]{:S(2)}) collective-permute-start(bf16[4,264,128]{2,1,0:T(8,128)(2,1)S(1)} %merge.1.refs_1_.refs_2_), channel_id=1, source_target_pairs={{0,3},{1,2},{2,1},{3,0},{4,7},{5,6},{6,5},{7,4},{8,11},{9,10},{10,... | collective-permute-start | bytes 811016 | tf_op jit(solution)/shard_map/ppermute | solution.py:248
  9.8 26.9 %collective-permute-start.7 = (bf16[4,264,128]{2,1,0:T(8,128)(2,1)S(1)}, bf16[4,264,128]{2,1,0:T(8,128)(2,1)S(1)}, u32[]{:S(2)}, u32[]{:S(2)}) collective-permute-start(bf16[4,264,128]{2,1,0:T(8,128)(2,1)S(1)} %merge.1.refs_1_.refs_2_), channel_id=1, source_target_pairs={{0,4},{4,0},{1,5},{5,1},{2,6},{6,2},{3,7},{7,3},{8,12},{12,8},{9,1... | collective-permute-start | bytes 811016 | tf_op jit(solution)/shard_map/ppermute | solution.py:268
  17.5 20.5 %collective-permute-start.8 = (bf16[4,264,128]{2,1,0:T(8,128)(2,1)S(1)}, bf16[4,264,128]{2,1,0:T(8,128)(2,1)S(1)}, u32[]{:S(2)}, u32[]{:S(2)}) collective-permute-start(bf16[4,264,128]{2,1,0:T(8,128)(2,1)S(1)} %collective-permute-done.6.refs_3_), channel_id=1, source_target_pairs={{0,4},{4,0},{1,5},{5,1},{2,6},{6,2},{3,7},{7,3},{8,12},{12,8},{9,1... | collective-permute-start | bytes 811016 | tf_op jit(solution)/shard_map/ppermute | solution.py:268
  19.8 35.1 %collective-permute-start.11 = (bf16[4,264,128]{2,1,0:T(8,128)(2,1)S(1)}, bf16[4,264,128]{2,1,0:T(8,128)(2,1)S(1)}, u32[]{:S(2)}, u32[]{:S(2)}) collective-permute-start(bf16[4,264,128]{2,1,0:T(8,128)(2,1)S(1)} %collective-permute-done.9.refs_2_), channel_id=1, source_target_pairs={{0,4},{4,0},{1,5},{5,1},{2,6},{6,2},{3,7},{7,3},{8,12},{12,8},{9,1... | collective-permute-start | bytes 811016 | tf_op jit(solution)/shard_map/ppermute | solution.py:268
  31.9 22.9 %collective-permute-start.12 = (bf16[4,264,128]{2,1,0:T(8,128)(2,1)S(1)}, bf16[4,264,128]{2,1,0:T(8,128)(2,1)S(1)}, u32[]{:S(2)}, u32[]{:S(2)}) collective-permute-start(bf16[4,264,128]{2,1,0:T(8,128)(2,1)S(1)} %collective-permute-done.10.refs_3_), channel_id=1, source_target_pairs={{0,4},{4,0},{1,5},{5,1},{2,6},{6,2},{3,7},{7,3},{8,12},{12,8},{9,1... | collective-permute-start | bytes 811016 | tf_op jit(solution)/shard_map/ppermute | solution.py:268
  35.9 8.9 %collective-permute-start.2 = (bf16[128,1024]{1,0:T(8,128)(2,1)S(1)}, bf16[128,1024]{1,0:T(8,128)(2,1)S(1)}, u32[]{:S(2)}, u32[]{:S(2)}) collective-permute-start(bf16[128,1024]{1,0:T(8,128)(2,1)S(1)} %get-tuple-element.39), channel_id=1, source_target_pairs={{0,24},{8,16},{16,8},{24,0},{1,25},{9,17},{17,9},{25,1},{2,26},{10... | collective-permute-start | bytes 786440 | tf_op jit(solution)/shard_map/ppermute | solution.py:248
  36.8 13.7 %collective-permute-start.1 = (bf16[128,1024]{1,0:T(8,128)(2,1)S(1)}, bf16[128,1024]{1,0:T(8,128)(2,1)S(1)}, u32[]{:S(2)}, u32[]{:S(2)}) collective-permute-start(bf16[128,1024]{1,0:T(8,128)(2,1)S(1)} %get-tuple-element.38), channel_id=1, source_target_pairs={{0,16},{8,24},{16,0},{24,8},{1,17},{9,25},{17,1},{25,9},{2,18},{10... | collective-permute-start | bytes 786440 | tf_op jit(solution)/shard_map/ppermute | solution.py:248
  38.0 13.5 %collective-permute-start = (bf16[128,1024]{1,0:T(8,128)(2,1)S(1)}, bf16[128,1024]{1,0:T(8,128)(2,1)S(1)}, u32[]{:S(2)}, u32[]{:S(2)}) collective-permute-start(bf16[128,1024]{1,0:T(8,128)(2,1)S(1)} %get-tuple-element.37), channel_id=1, source_target_pairs={{0,8},{8,0},{16,24},{24,16},{1,9},{9,1},{17,25},{25,17},{2,10},{10... | collective-permute-start | bytes 786440 | tf_op jit(solution)/shard_map/ppermute | solution.py:248
  59.9 9.5 %collective-permute-start.13 = (bf16[128,1024]{1,0:T(8,128)(2,1)S(1)}, bf16[128,1024]{1,0:T(8,128)(2,1)S(1)}, u32[]{:S(2)}, u32[]{:S(2)}) collective-permute-start(bf16[128,1024]{1,0:T(8,128)(2,1)S(1)} %attend.16), channel_id=1, source_target_pairs={{0,8},{8,0},{16,24},{24,16},{1,9},{9,1},{17,25},{25,17},{2,10},{10... | collective-permute-start | bytes 786440 | tf_op jit(solution)/shard_map/ppermute | solution.py:248
  62.5 12.6 %collective-permute-start.14 = (bf16[128,1024]{1,0:T(8,128)(2,1)S(1)}, bf16[128,1024]{1,0:T(8,128)(2,1)S(1)}, u32[]{:S(2)}, u32[]{:S(2)}) collective-permute-start(bf16[128,1024]{1,0:T(8,128)(2,1)S(1)} %attend.15), channel_id=1, source_target_pairs={{0,16},{8,24},{16,0},{24,8},{1,17},{9,25},{17,1},{25,9},{2,18},{10... | collective-permute-start | bytes 786440 | tf_op jit(solution)/shard_map/ppermute | solution.py:248
  63.1 12.0 %collective-permute-start.15 = (bf16[128,1024]{1,0:T(8,128)(2,1)S(1)}, bf16[128,1024]{1,0:T(8,128)(2,1)S(1)}, u32[]{:S(2)}, u32[]{:S(2)}) collective-permute-start(bf16[128,1024]{1,0:T(8,128)(2,1)S(1)} %attend.14), channel_id=1, source_target_pairs={{0,24},{8,16},{16,8},{24,0},{1,25},{9,17},{17,9},{25,1},{2,26},{10... | collective-permute-start | bytes 786440 | tf_op jit(solution)/shard_map/ppermute | solution.py:248
